TPU v7x, 32 devices: a whole 2x2x4 slice. The times are simulated.
32 devices in a mesh: gx: 2 (over x), gy: 4 (over y, core), gz: 4 (over z).
Axes of the slice: x: 2, y: 2, z: 4, core: 2. Of those that a mesh axis runs over, the one named last changes fastest.
Arguments:
- features: bfloat16 [256, 4096], P('gz', ('gy', 'gx')), may hold values from -14 to 14, as said below
- tiles: bfloat16 [32, 32, 128, 128], P('gx', 'gy'), may hold values from -0.5 to 0.5
- block_mask: int32 [32, 32], P('gx', 'gy'), may hold values from 0 to 1, as said below
- tile_counts: int32 [32], P('gx'), may hold values from 1 to 32, as said below
- weight: bfloat16 [256, 256], replicated, may hold values from -0.375 to 0.375
- gamma: float32 [256], P('gz'), may hold values from 0.5 to 2
- beta: float32 [256], P('gz'), may hold values from -3 to 3
Outputs:
- normed: bfloat16 [256, 4096], P('gz', ('gx', 'gy'))
Inputs may be any that keep to these rules, and one draw needn't show every extreme that they name: `features`: channels along dimension 0, nodes along dimension 1. `block_mask`: 1 where block row and block column meet in a nonzero block, else 0; the diagonal is 1. tile_counts[r] is the number of ones in row r of block_mask.
All inputs are finite; a program needn't handle non-finite values.
Results may differ from a plain program's by a relative error of at most 0.013.
Values may be sent and summed in bfloat16 or wider, within the bound.
A program may use at most 64 MiB of HBM per device.

v0:
```python
import jax
import jax.numpy as jnp
from jax import lax
from jax.sharding import PartitionSpec as P


def body(features, tiles, block_mask, tile_counts, weight, gamma, beta):
    panel = lax.all_gather(features, "gx", axis=1, tiled=True)
    local_ch = panel.shape[0]
    rows_blk = tiles.shape[0]
    cols_blk = tiles.shape[1]
    tile_len = tiles.shape[2]
    panels = panel.reshape(local_ch, cols_blk, tile_len)
    prods = jnp.einsum("fcn,rcmn->frcm", panels, tiles, preferred_element_type=jnp.float32)
    share = block_mask.astype(jnp.float32) / tile_counts.astype(jnp.float32)[:, None]
    partial_value = jnp.einsum("frcm,rc->frm", prods, share).reshape(local_ch, rows_blk * tile_len)
    summed = lax.psum(partial_value, "gy")
    width = rows_blk * tile_len // lax.axis_size("gy")
    agg = lax.dynamic_slice_in_dim(summed, lax.axis_index("gy") * width, width, 1)
    agg = agg.astype(jnp.bfloat16)
    offset = lax.axis_index("gz") * local_ch
    full = lax.all_gather(agg, "gz", axis=0, tiled=True)
    w_cols = lax.dynamic_slice_in_dim(weight, offset, local_ch, 1)
    z_vals = jnp.einsum("co,cn->on", w_cols, full, preferred_element_type=jnp.float32)
    total = z_vals.shape[1] * lax.axis_size(("gx", "gy"))
    sums, squares = lax.psum(
        (jnp.sum(z_vals, axis=1), jnp.sum(z_vals * z_vals, axis=1)), ("gx", "gy")
    )
    mean = sums / total
    var = squares / total - mean * mean
    centered = z_vals - mean[:, None]
    scaled = gamma[:, None] * centered * lax.rsqrt(var + 1e-05)[:, None] + beta[:, None]
    return jnp.maximum(scaled, 0.0).astype(jnp.bfloat16)


def solution(mesh):
    in_specs = (
        P("gz", ("gy", "gx")),
        P("gx", "gy", None, None),
        P("gx", "gy"),
        P("gx"),
        P(),
        P("gz"),
        P("gz"),
    )
    out_specs = P("gz", ("gx", "gy"))
    return jax.shard_map(body, mesh=mesh, in_specs=in_specs, out_specs=out_specs, check_vma=False)
```

profile of v0, /device:TPU:0, one launch (start us, length us, event | category | flops | bytes accessed | tf_op | source)
XLA Modules:
  0.0 57.3 jit_solution(9171550169248883873)
XLA Ops:
  0.0 0.0 copy-start
  0.0 0.7 %convert_element_type.13 = f32[16]{0:T(128)S(1)} convert(s32[16]{0:T(128)} %param.10) | non-fusion elementwise | flops 16 | bytes 128 | tf_op jit(solution)/shard_map/convert_element_type | solution.py:15
  0.7 0.7 %divide_bitcast_fusion = bf16[16,8,1,1]{0,1,2,3:T(8,128)(2,1)S(1)} fusion(s32[16,8]{0,1:T(8,128)} %param.9, f32[16]{0:T(128)S(1)} %convert_element_type.13), kind=kLoop, calls=%fused_computation.12 | loop fusion | flops 384 | bytes 832 | tf_op jit(solution)/shard_map/div | solution.py:15
  1.4 0.1 copy.12
  1.5 6.1 %all_gather.6 = bf16[64,1024]{1,0:T(8,128)(2,1)S(1)} all-gather(bf16[64,512]{1,0:T(8,128)(2,1)} %param.7), channel_id=1, replica_groups=mesh['gx'=2,'gy'=4,'gz'=4] {'gx'}, dimensions={1}, use_global_device_ids=true | all-gather | bytes 196608 | tf_op jit(solution)/shard_map/all_gather | solution.py:8
  7.6 3.8 %fusion.4 = bf16[64,16,8,128]{3,0,1,2:T(8,128)(2,1)S(1)} fusion(bf16[16,8,128,128]{3,2,1,0:T(8,128)(2,1)} %param.8, bf16[64,8,128,1]{2,1,0,3:T(8,128)(2,1)S(1)} %bitcast.19), kind=kOutput, calls=%fused_computation.4 | convolution fusion | flops 268435456 | bytes 6422528 | tf_op jit(solution)/shard_map/fcn,rcmn->frcm/dot_general | solution.py:14
  11.4 1.4 %fusion = f32[16,1,64,128]{3,1,2,0:T(1,128)S(1)} fusion(bf16[16,8,1,1]{1,2,3,0:T(2,128)(2,1)S(1)} %copy.12, bf16[64,16,8,128]{3,0,1,2:T(8,128)(2,1)S(1)} %fusion.4), kind=kOutput, calls=%fused_computation | convolution fusion | flops 2097152 | bytes 2621696 | tf_op jit(solution)/shard_map/frcm,rc->frm/dot_general | solution.py:16
  12.8 0.0 copy-start.1
  12.8 0.0 copy-start.2
  12.8 0.3 copy.14
  13.2 0.2 copy.28
  13.3 16.7 %all-reduce.2 = bf16[64,2048]{1,0:T(8,128)(2,1)S(1)} all-reduce(f32[64,2048]{1,0:T(8,128)S(1)} %bitcast.18), channel_id=1, replica_groups=mesh['gx'=2,'gy'=4,'gz'=4] {'gy'}, use_global_device_ids=true, to_apply=%region_0.0 | all-reduce | flops 131072 | bytes 786432 | tf_op jit(solution)/shard_map/psum | solution.py:17
  30.1 14.2 %all_gather.7 = bf16[256,512]{1,0:T(8,128)(2,1)S(1)} all-gather(bf16[64,512]{1,0:T(8,128)(2,1)S(1)} %dynamic-slice_convert_fusion), channel_id=1, replica_groups=mesh['gx'=2,'gy'=4,'gz'=4] {'gz'}, dimensions={0}, use_global_device_ids=true | all-gather | bytes 327680 | tf_op jit(solution)/shard_map/all_gather | solution.py:22
  44.3 0.0 copy-done
  44.3 0.4 fusion.11
  44.7 11.8 %all-reduce = (f32[64]{0:T(128)S(1)}, f32[64]{0:T(128)S(1)}) all-reduce(f32[64]{0:T(128)S(1)} %get-tuple-element.6, f32[64]{0:T(128)S(1)} %get-tuple-element.5), channel_id=1, replica_groups=mesh['gx'=2,'gy'=4,'gz'=4] {'gx','gy'}, use_global_device_ids=true, to_apply=%region_4.0 | all-reduce | flops 128 | bytes 1024 | tf_op jit(solution)/shard_map/psum | solution.py:26
  56.5 0.0 copy-done.1
  56.5 0.0 copy-done.2
  56.5 0.7 %maximum_convert_fusion = bf16[64,512]{1,0:T(8,128)(2,1)} fusion(f32[64,512]{1,0:T(8,128)S(1)} %get-tuple-element.11, f32[64]{0:T(128)S(1)} %copy-done.1, f32[64]{0:T(128)S(1)} %get-tuple-element.10, f32[64]{0:T(128)S(1)} %get-tuple-element.9, f32[64]{0:T(128)S(1)} %copy-done.2), kind=kLoop, calls=%fused_computation.7 | loop fusion | flops 196608 | bytes 197632 | tf_op jit(solution)/shard_map/convert_element_type | solution.py:33
  (3 shorter events, 0.0 us)
Async XLA Ops:
  0.0 44.3 %copy-start = (bf16[256,256]{1,0:T(8,128)(2,1)S(1)}, bf16[256,256]{1,0:T(8,128)(2,1)}, u32[]{:S(2)}) copy-start(bf16[256,256]{1,0:T(8,128)(2,1)} %param.11) | copy-start | bytes 393220
  12.8 43.7 %copy-start.1 = (f32[64]{0:T(128)S(1)}, f32[64]{0:T(128)}, u32[]{:S(2)}) copy-start(f32[64]{0:T(128)} %param.13) | copy-start | bytes 772
  12.8 43.7 %copy-start.2 = (f32[64]{0:T(128)S(1)}, f32[64]{0:T(128)}, u32[]{:S(2)}) copy-start(f32[64]{0:T(128)} %param.12) | copy-start | bytes 772
where the time goes:
time: 57.5 us; the launch traced here: 57.3 us
  blocking collectives  48.9 us (85%)
  matrix products  5.54 us (10%)
  other arithmetic  2.13 us (4%)
  local copies, waits for them, and re-layouts  0.61 us (1%)
    psum x1, blocking collectives, body(): summed = lax.psum(partial_value, 'gy')  16.7 us
    all_gather x1, blocking collectives, body(): full = lax.all_gather(agg, 'gz', axis=0, tiled=True)  14.2 us
    psum x1, blocking collectives, body(): lax.psum((jnp.sum(z_vals, axis=1), jnp.sum(z_vals * z_vals, axis=1)), ('g...  11.8 us
    all_gather x1, blocking collectives, body(): panel = lax.all_gather(features, 'gx', axis=1, tiled=True)  6.13 us
    dot_general x1, matrix products, body(): jnp.einsum('fcn,rcmn->frcm', panels, tiles, preferred_element_type=jnp.fl...  3.75 us
    dot_general x1, matrix products, body(): jnp.einsum('frcm,rc->frm', prods, share)  1.42 us

commit v1 on v0

--- a/solution.py
+++ b/solution.py
@@ -19,9 +19,42 @@
     agg = lax.dynamic_slice_in_dim(summed, lax.axis_index("gy") * width, width, 1)
     agg = agg.astype(jnp.bfloat16)
     offset = lax.axis_index("gz") * local_ch
-    full = lax.all_gather(agg, "gz", axis=0, tiled=True)
     w_cols = lax.dynamic_slice_in_dim(weight, offset, local_ch, 1)
-    z_vals = jnp.einsum("co,cn->on", w_cols, full, preferred_element_type=jnp.float32)
+    part_next = lax.axis_size("gz")
+    local_next = lax.axis_index("gz")
+    q_next, carry_out, tile_out = (part_next, local_next, agg.shape[0])
+    pile = [(hop_no, (hop_no + 1) % q_next) for hop_no in range(q_next)]
+    by_rank = [(hop_no, (hop_no - 1) % q_next) for hop_no in range(q_next)]
+    finding = q_next // 2
+    row_out = left_arr = agg
+    z_vals = jnp.einsum(
+        "co,cn->on",
+        lax.dynamic_slice_in_dim(w_cols, carry_out * tile_out, agg.shape[0], axis=0),
+        agg,
+        preferred_element_type=jnp.float32,
+    )
+    for i in range(1, finding + 1):
+        row_out = lax.ppermute(row_out, "gz", pile)
+        if i < q_next - finding:
+            left_arr = lax.ppermute(left_arr, "gz", by_rank)
+            met_up = jnp.einsum(
+                "co,cn->on",
+                lax.dynamic_slice_in_dim(
+                    w_cols, (carry_out + i) % q_next * tile_out, left_arr.shape[0], axis=0
+                ),
+                left_arr,
+                preferred_element_type=jnp.float32,
+            )
+            z_vals = z_vals + met_up
+        r_now = jnp.einsum(
+            "co,cn->on",
+            lax.dynamic_slice_in_dim(
+                w_cols, (carry_out - i) % q_next * tile_out, row_out.shape[0], axis=0
+            ),
+            row_out,
+            preferred_element_type=jnp.float32,
+        )
+        z_vals = z_vals + r_now
     total = z_vals.shape[1] * lax.axis_size(("gx", "gy"))
     sums, squares = lax.psum(
         (jnp.sum(z_vals, axis=1), jnp.sum(z_vals * z_vals, axis=1)), ("gx", "gy")

time: 57.5 us -> 59.2 us (1.030)
  blocking collectives: 48.9 us -> 34.7 us
  waiting for transfers between devices: 0 us -> 11.2 us
  starting transfers between devices: 0 us -> 3.76 us
  matrix products: 5.54 us -> 6.34 us
    all_gather x1 -> x0, blocking collectives: 14.2 us -> none  [body(): full = lax.all_gather(agg, 'gz', axis=0, tiled=True)]
    ppermute x0 -> x3, waiting for transfers between devices: none -> 11.2 us  [the longest x2 11.2 us: body(): row_out = lax.ppermute(row_out, 'gz', pile)]
    ppermute x0 -> x3, starting transfers between devices: none -> 3.76 us  [the longest x1 3.76 us: body(): left_arr = lax.ppermute(left_arr, 'gz', by_rank)]
    dot_general x1 -> x4, matrix products: 0.37 us -> 1.17 us  [the longest x2 0.65 us: body(): jnp.einsum('co,cn->on', lax.dynamic_slice_in_dim(w_cols, (carry_out - i)...]
  transfers between devices with their start and end apart: 0 -> 3, of which waited for: 0 -> 2; matrix products, arithmetic and copies ran while one was open for 0% -> 1% of each run, Pallas kernels for 0% -> 0%
where the time goes in v1:
time: 59.2 us; the launch traced here: 58.9 us
  blocking collectives  34.7 us (59%)
  waiting for transfers between devices  11.2 us (19%)
  matrix products  6.34 us (11%)
  starting transfers between devices  3.76 us (6%)
  other arithmetic  2.13 us (4%)
  local copies, waits for them, and re-layouts  0.61 us (1%)
    psum x1, blocking collectives, body(): summed = lax.psum(partial_value, 'gy')  16.7 us
    psum x1, blocking collectives, body(): lax.psum((jnp.sum(z_vals, axis=1), jnp.sum(z_vals * z_vals, axis=1)), ('g...  11.8 us
    ppermute x2, waiting for transfers between devices, body(): row_out = lax.ppermute(row_out, 'gz', pile)  11.2 us
    all_gather x1, blocking collectives, body(): panel = lax.all_gather(features, 'gx', axis=1, tiled=True)  6.13 us
    ppermute x1, starting transfers between devices, body(): left_arr = lax.ppermute(left_arr, 'gz', by_rank)  3.76 us
    dot_general x1, matrix products, body(): jnp.einsum('fcn,rcmn->frcm', panels, tiles, preferred_element_type=jnp.fl...  3.75 us
    dot_general x1, matrix products, body(): jnp.einsum('frcm,rc->frm', prods, share)  1.42 us
  transfers between devices with their start and end apart: 3, of which 2 were waited for; matrix products, arithmetic and copies ran while one was open for 1% of the time, Pallas kernels for 0%

profile of v1, /device:TPU:0, one launch (start us, length us, event | category | flops | bytes accessed | tf_op | source)
XLA Modules:
  0.0 58.9 jit_solution(16422485487506168689)
XLA Ops:
  0.0 0.0 copy-start
  0.0 0.7 %convert_element_type.13 = f32[16]{0:T(128)S(1)} convert(s32[16]{0:T(128)} %param.10) | non-fusion elementwise | flops 16 | bytes 128 | tf_op jit(solution)/shard_map/convert_element_type | solution.py:15
  0.7 0.7 %divide_bitcast_fusion = bf16[16,8,1,1]{0,1,2,3:T(8,128)(2,1)S(1)} fusion(s32[16,8]{0,1:T(8,128)} %param.9, f32[16]{0:T(128)S(1)} %convert_element_type.13), kind=kLoop, calls=%fused_computation.18 | loop fusion | flops 384 | bytes 832 | tf_op jit(solution)/shard_map/div | solution.py:15
  1.4 0.1 copy.12
  1.5 6.1 %all_gather.3 = bf16[64,1024]{1,0:T(8,128)(2,1)S(1)} all-gather(bf16[64,512]{1,0:T(8,128)(2,1)} %param.7), channel_id=1, replica_groups=mesh['gx'=2,'gy'=4,'gz'=4] {'gx'}, dimensions={1}, use_global_device_ids=true | all-gather | bytes 196608 | tf_op jit(solution)/shard_map/all_gather | solution.py:8
  7.6 3.8 %fusion.4 = bf16[64,16,8,128]{3,0,1,2:T(8,128)(2,1)S(1)} fusion(bf16[16,8,128,128]{3,2,1,0:T(8,128)(2,1)} %param.8, bf16[64,8,128,1]{2,1,0,3:T(8,128)(2,1)S(1)} %bitcast.22), kind=kOutput, calls=%fused_computation.4 | convolution fusion | flops 268435456 | bytes 6422528 | tf_op jit(solution)/shard_map/fcn,rcmn->frcm/dot_general | solution.py:14
  11.4 1.4 %fusion = f32[16,1,64,128]{3,1,2,0:T(1,128)S(1)} fusion(bf16[16,8,1,1]{1,2,3,0:T(2,128)(2,1)S(1)} %copy.12, bf16[64,16,8,128]{3,0,1,2:T(8,128)(2,1)S(1)} %fusion.4), kind=kOutput, calls=%fused_computation | convolution fusion | flops 2097152 | bytes 2621696 | tf_op jit(solution)/shard_map/frcm,rc->frm/dot_general | solution.py:16
  12.8 0.0 copy-start.1
  12.8 0.0 copy-start.2
  12.8 0.3 copy.14
  13.2 0.2 copy.28
  13.3 16.7 %all-reduce.2 = bf16[64,2048]{1,0:T(8,128)(2,1)S(1)} all-reduce(f32[64,2048]{1,0:T(8,128)S(1)} %bitcast.21), channel_id=1, replica_groups=mesh['gx'=2,'gy'=4,'gz'=4] {'gy'}, use_global_device_ids=true, to_apply=%region_0.0 | all-reduce | flops 131072 | bytes 786432 | tf_op jit(solution)/shard_map/psum | solution.py:17
  30.1 3.8 %collective-permute-start = (bf16[64,512]{1,0:T(8,128)(2,1)S(1)}, bf16[64,512]{1,0:T(8,128)(2,1)S(1)}, u32[]{:S(2)}, u32[]{:S(2)}) collective-permute-start(bf16[64,512]{1,0:T(8,128)(2,1)S(1)} %dynamic-slice_convert_fusion), channel_id=1, source_target_pairs={{0,3},{1,0},{2,1},{3,2},{4,7},{5,4},{6,5},{7,6},{8,11},{9,8},{10,9... | collective-permute-start | bytes 196616 | tf_op jit(solution)/shard_map/ppermute | solution.py:39
  33.9 0.0 collective-permute-start.1
  33.9 0.0 copy-done
  33.9 0.3 fusion.11
  34.2 5.7 %collective-permute-done.1 = bf16[64,512]{1,0:T(8,128)(2,1)S(1)} collective-permute-done((bf16[64,512]{1,0:T(8,128)(2,1)S(1)}, bf16[64,512]{1,0:T(8,128)(2,1)S(1)}, u32[]{:S(2)}, u32[]{:S(2)}) %collective-permute-start.1) | collective-permute-done | bytes 65568 | tf_op jit(solution)/shard_map/ppermute | solution.py:37
  39.9 0.0 collective-permute-start.2
  39.9 0.0 collective-permute-done
  39.9 0.3 convolution_add_fusion.2
  40.2 0.3 convolution_add_fusion.1
  40.5 5.5 %collective-permute-done.2 = bf16[64,512]{1,0:T(8,128)(2,1)S(1)} collective-permute-done((bf16[64,512]{1,0:T(8,128)(2,1)S(1)}, bf16[64,512]{1,0:T(8,128)(2,1)S(1)}, u32[]{:S(2)}, u32[]{:S(2)}) %collective-permute-start.2) | collective-permute-done | bytes 65568 | tf_op jit(solution)/shard_map/ppermute | solution.py:37
  46.0 0.4 fusion.13
  46.4 11.8 %all-reduce = (f32[64]{0:T(128)S(1)}, f32[64]{0:T(128)S(1)}) all-reduce(f32[64]{0:T(128)S(1)} %get-tuple-element.6, f32[64]{0:T(128)S(1)} %get-tuple-element.5), channel_id=1, replica_groups=mesh['gx'=2,'gy'=4,'gz'=4] {'gx','gy'}, use_global_device_ids=true, to_apply=%region_4.5 | all-reduce | flops 128 | bytes 1024 | tf_op jit(solution)/shard_map/psum | solution.py:59
  58.2 0.0 copy-done.1
  58.2 0.0 copy-done.2
  58.2 0.7 %maximum_convert_fusion = bf16[64,512]{1,0:T(8,128)(2,1)} fusion(f32[64,512]{1,0:T(8,128)S(1)} %get-tuple-element.11, f32[64]{0:T(128)S(1)} %copy-done.1, f32[64]{0:T(128)S(1)} %get-tuple-element.10, f32[64]{0:T(128)S(1)} %get-tuple-element.9, f32[64]{0:T(128)S(1)} %copy-done.2), kind=kLoop, calls=%fused_computation.10 | loop fusion | flops 196608 | bytes 197632 | tf_op jit(solution)/shard_map/convert_element_type | solution.py:66
  (3 shorter events, 0.0 us)
Async XLA Ops:
  0.0 33.9 %copy-start = (bf16[256,256]{1,0:T(8,128)(2,1)S(1)}, bf16[256,256]{1,0:T(8,128)(2,1)}, u32[]{:S(2)}) copy-start(bf16[256,256]{1,0:T(8,128)(2,1)} %param.11) | copy-start | bytes 393220
  12.8 45.4 %copy-start.1 = (f32[64]{0:T(128)S(1)}, f32[64]{0:T(128)}, u32[]{:S(2)}) copy-start(f32[64]{0:T(128)} %param.13) | copy-start | bytes 772
  12.8 45.4 %copy-start.2 = (f32[64]{0:T(128)S(1)}, f32[64]{0:T(128)}, u32[]{:S(2)}) copy-start(f32[64]{0:T(128)} %param.12) | copy-start | bytes 772
  30.1 9.8 %collective-permute-start = (bf16[64,512]{1,0:T(8,128)(2,1)S(1)}, bf16[64,512]{1,0:T(8,128)(2,1)S(1)}, u32[]{:S(2)}, u32[]{:S(2)}) collective-permute-start(bf16[64,512]{1,0:T(8,128)(2,1)S(1)} %dynamic-slice_convert_fusion), channel_id=1, source_target_pairs={{0,3},{1,0},{2,1},{3,2},{4,7},{5,4},{6,5},{7,6},{8,11},{9,8},{10,9... | collective-permute-start | bytes 196616 | tf_op jit(solution)/shard_map/ppermute | solution.py:39
  33.9 6.1 %collective-permute-start.1 = (bf16[64,512]{1,0:T(8,128)(2,1)S(1)}, bf16[64,512]{1,0:T(8,128)(2,1)S(1)}, u32[]{:S(2)}, u32[]{:S(2)}) collective-permute-start(bf16[64,512]{1,0:T(8,128)(2,1)S(1)} %dynamic-slice_convert_fusion), channel_id=1, source_target_pairs={{0,1},{1,2},{2,3},{3,0},{4,5},{5,6},{6,7},{7,4},{8,9},{9,10},{10,1... | collective-permute-start | bytes 196616 | tf_op jit(solution)/shard_map/ppermute | solution.py:37
  39.9 6.1 %collective-permute-start.2 = (bf16[64,512]{1,0:T(8,128)(2,1)S(1)}, bf16[64,512]{1,0:T(8,128)(2,1)S(1)}, u32[]{:S(2)}, u32[]{:S(2)}) collective-permute-start(bf16[64,512]{1,0:T(8,128)(2,1)S(1)} %collective-permute-done.1), channel_id=1, source_target_pairs={{0,1},{1,2},{2,3},{3,0},{4,5},{5,6},{6,7},{7,4},{8,9},{9,10},{10,1... | collective-permute-start | bytes 196616 | tf_op jit(solution)/shard_map/ppermute | solution.py:37
